TPU v7x, 32 devices: a whole 2x2x4 slice. The times are simulated.
32 devices in a mesh: rows: 4 (over z), vocab: 8 (over y, x, core).
Axes of the slice: x: 2, y: 2, z: 4, core: 2. Of those that a mesh axis runs over, the one named last changes fastest.
Arguments:
- hidden: bfloat16 [512, 8192], P('rows', 'vocab'), may hold values from -30 to 30
- head: bfloat16 [8192, 152064], P(None, ('vocab', 'rows')), may hold values from -1 to 1
- states: int32 [512], replicated, may hold values from 0 to 2047
- class_of: int32 [152064], P('vocab'), may hold values from 0 to 255, as said below
- table: int32 [2048, 8], replicated, may hold values from -2147483648 to 2147483646, as said below
Outputs:
- log_probs: float32 [512, 152064], P('rows', 'vocab')
- entropy: float32 [512], P('rows')
Inputs may be any that keep to these rules, and one draw needn't show every extreme that they name: `class_of`: class 0 is the class of at least one token. `table`: bit 0 of word 0 is set in every state, so class 0 is allowed everywhere.
All inputs are finite; a program needn't handle non-finite values.
Results may differ from a plain program's by a relative error of at most 0.0003.
Values may be sent and summed in bfloat16 or wider, within the bound.
A program may use at most 192 MiB of HBM per device.

v0:
```python
import jax
import jax.numpy as jnp
from jax import lax
from jax.sharding import PartitionSpec as P

masked_floor = -1e30


def token_mask(states, table, class_of):
    words = jnp.take(table, states, axis=0)
    shifts = lax.broadcasted_iota(jnp.int32, (1, 1, 32), 2)
    bit_values = jnp.bitwise_and(jnp.right_shift(words[:, :, None], shifts), 1)
    allowed_class = bit_values.reshape(words.shape[0], words.shape[1] * 32).astype(jnp.bfloat16)
    onehot = (
        lax.broadcasted_iota(jnp.int32, (allowed_class.shape[1], class_of.shape[0]), 0)
        == class_of[None, :]
    ).astype(jnp.bfloat16)
    return jnp.dot(allowed_class, onehot, preferred_element_type=jnp.float32) > 0.5


def masked_peak(logits, allowed):
    return jnp.max(jnp.where(allowed, logits, masked_floor), axis=1)


def weighted_sums(logits, allowed, peak):
    weights = jnp.where(allowed, jnp.exp(logits - peak[:, None]), 0.0)
    return (jnp.sum(weights, axis=1), jnp.sum(weights * logits, axis=1))


def finish(logits, allowed, peak, total, weighted):
    norm_log = peak + jnp.log(total)
    log_probs = jnp.where(allowed, logits - norm_log[:, None], 0.0)
    return (log_probs, norm_log - weighted / total)


def vocab_stats(logits, allowed):
    own_peak = masked_peak(logits, allowed)
    own_total, own_weighted = weighted_sums(logits, allowed, own_peak)
    parts = lax.all_gather(jnp.stack([own_peak, own_total, own_weighted]), "vocab", axis=0)
    peak = jnp.max(parts[:, 0], axis=0)
    factor = jnp.exp(parts[:, 0] - peak[None, :])
    return (peak, jnp.sum(factor * parts[:, 1], axis=0), jnp.sum(factor * parts[:, 2], axis=0))


levels = 65000.0


def encode(logits):
    high = jnp.max(logits, axis=1)
    low = jnp.min(logits, axis=1)
    middle = 0.5 * (high + low)
    width = jnp.maximum(high - low, 1e-30)
    scaled = (logits - middle[:, None]) * (levels / width)[:, None]
    return (
        jnp.round(scaled).astype(jnp.int32).astype(jnp.int16),
        jnp.stack([middle, width / levels], axis=1),
    )


def to_row_groups(logits):
    groups = lax.axis_size("rows")
    rows, columns = logits.shape
    own = rows // groups
    codes, scales = encode(logits)
    codes = lax.all_to_all(codes.reshape(groups, own, columns), "rows", 0, 0)
    scales = lax.all_to_all(scales.reshape(groups, own, 2), "rows", 0, 0)
    values = codes.astype(jnp.float32) * scales[:, :, 1:2] + scales[:, :, 0:1]
    return jnp.transpose(values, (1, 0, 2)).reshape(own, groups * columns)


def on_device(hidden, head, states, class_of, table):
    all_rows = lax.all_gather(hidden, "rows", axis=0, tiled=True)
    logits = jnp.dot(
        lax.all_gather(all_rows, "vocab", axis=1, tiled=True),
        head,
        preferred_element_type=jnp.float32,
    )
    group = lax.axis_index("rows")
    own_count = states.shape[0] // lax.axis_size("rows")
    own_logits = to_row_groups(logits)
    own_states = lax.dynamic_slice_in_dim(states, group * own_count, own_count, 0)
    allowed = token_mask(own_states, table, class_of)
    peak, total, weighted = vocab_stats(own_logits, allowed)
    log_probs, entropy = finish(own_logits, allowed, peak, total, weighted)
    return (log_probs, entropy)


def solution(mesh):
    in_specs = (P("rows", "vocab"), P(None, ("vocab", "rows")), P(), P("vocab"), P())
    out_specs = (P("rows", "vocab"), P("rows"))
    return jax.shard_map(
        on_device, mesh=mesh, in_specs=in_specs, out_specs=out_specs, check_vma=False
    )
```

profile of v0, /device:TPU:0, one launch (start us, length us, event | category | flops | bytes accessed | tf_op | source)
XLA Modules:
  0.0 309.3 jit_solution(13070469323877328229)
XLA Ops:
  7.2 0.0 all-gather.5.cloned.1.call-start
  7.2 0.7 all-gather.5.cloned.1.call-update
  7.9 0.0 all-gather.7.cloned.1.call-start
  7.9 32.3 %all-gather.5.cloned.1.call-done = bf16[512,1024]{1,0:T(8,128)(2,1)} async-done(((bf16[128,1024]{1,0:T(8,128)(2,1)}), bf16[512,1024]{1,0:T(8,128)(2,1)}) %all-gather.5.cloned.1.call-update) | async-done | bytes 1048592 | tf_op jit(solution)/shard_map/all_gather | solution.py:72
  40.3 0.0 all-gather.7.cloned.1.call-update
  40.3 55.5 %all-gather.7.cloned.1.call-done = bf16[512,8192]{1,0:T(8,128)(2,1)} async-done(((bf16[512,1024]{1,0:T(8,128)(2,1)}), bf16[512,8192]{1,0:T(8,128)(2,1)}) %all-gather.7.cloned.1.call-update) | async-done | bytes 8388624 | tf_op jit(solution)/shard_map/all_gather | solution.py:74
  95.9 49.4 %fusion.10 = (f32[512]{0:T(512)S(1)}, f32[512]{0:T(512)S(1)}, f32[512,4752]{0,1:T(8,128)}) fusion(bf16[512,8192]{1,0:T(8,128)(2,1)} %all-gather.7.cloned.1.call-done, bf16[8192,4752]{0,1:T(8,128)(2,1)} %param.6), kind=kOutput, calls=%fused_computation.36 | convolution fusion | flops 39867531264 | bytes 95981568 | tf_op jit(solution)/shard_map/dot_general | solution.py:73
  145.3 0.6 pad_maximum_fusion
  145.9 4.6 %all-to-all-start.1 = ((f32[4,128,2]{1,2,0:T(2,128)}), f32[4,128,2]{1,2,0:T(2,128)S(1)}, u32[]{:S(2)}, u32[]{:S(2)}) async-start(f32[4,128,2]{1,2,0:T(2,128)} %pad_maximum_fusion), calls=%async_computation.1 | async-start | bytes 8192 | tf_op jit(solution)/shard_map/all_to_all | solution.py:66
  150.5 0.0 copy-start.1
  150.5 7.2 %copy_bitcast_fusion = s16[4,128,4752]{1,2,0:T(8,128)(2,1)} fusion(f32[512,4752]{0,1:T(8,128)} %get-tuple-element.20, f32[512]{0:T(512)S(1)} %get-tuple-element.16, f32[512]{0:T(512)S(1)} %get-tuple-element.17), kind=kLoop, calls=%fused_computation.17 | loop fusion | flops 12165120 | bytes 14602240 | tf_op jit(solution)/shard_map/reshape | solution.py:65
  157.7 0.0 all-to-all-done.1
  157.7 5.2 %all-to-all-start = ((s16[4,128,4752]{1,2,0:T(8,128)(2,1)}), s16[4,128,4752]{1,2,0:T(8,128)(2,1)}, u32[]{:S(2)}, u32[]{:S(2)}) async-start(s16[4,128,4752]{1,2,0:T(8,128)(2,1)} %copy_bitcast_fusion), calls=%async_computation | async-start | bytes 9732096 | tf_op jit(solution)/shard_map/all_to_all | solution.py:65
  162.9 0.0 copy-start.2
  162.9 0.1 shift_right_arithmetic.23
  163.0 0.0 copy-done.1
  163.0 0.3 copy.16
  163.4 0.8 compare_and_fusion
  164.1 0.6 gather_fusion
  164.8 0.1 broadcast_select_fusion
  164.9 0.1 fusion.9
  165.1 105.9 %all-to-all-done = s16[4,128,4752]{1,2,0:T(8,128)(2,1)} async-done(((s16[4,128,4752]{1,2,0:T(8,128)(2,1)}), s16[4,128,4752]{1,2,0:T(8,128)(2,1)}, u32[]{:S(2)}, u32[]{:S(2)}) %all-to-all-start) | async-done | bytes 4866080 | tf_op jit(solution)/shard_map/all_to_all | solution.py:65
  270.9 4.3 %multiply_add_fusion = f32[4,128,4752]{1,2,0:T(8,128)S(1)} fusion(s16[4,128,4752]{1,2,0:T(8,128)(2,1)} %all-to-all-done, f32[4,128]{1,0:T(4,128)S(1)} %bitcast.57, f32[4,128]{1,0:T(4,128)S(1)} %bitcast.56), kind=kLoop, calls=%fused_computation.14 | loop fusion | flops 7299072 | bytes 14602240 | tf_op jit(solution)/shard_map/add | solution.py:67
  275.2 0.0 copy-done.2
  275.2 0.0 copy-start
  275.2 6.1 %fusion.1 = (f32[128]{0:T(128)S(1)}, pred[128,19008]{0,1:T(8,128)(4,1)S(1)}) fusion(f32[4,128,4752]{1,2,0:T(8,128)S(1)} %multiply_add_fusion, bf16[128,256]{0,1:T(8,128)(2,1)S(1)} %fusion.9, s32[19008]{0:T(1024)S(1)} %copy-done.2), kind=kOutput, calls=%fused_computation.8 | convolution fusion | flops 1257873280 | bytes 12307200 | tf_op jit(solution)/shard_map/dot_general | solution.py:18
  281.3 0.0 copy-done
  281.3 2.9 fusion.4
  284.2 8.9 %all-gather.1 = f32[8,3,128]{2,1,0:T(4,128)S(1)} all-gather(f32[1,3,128]{2,1,0:T(4,128)S(1)} %maximum_bitcast_fusion), channel_id=2, replica_groups=mesh['rows'=4,'vocab'=8] {'vocab'}, dimensions={0}, use_global_device_ids=true | all-gather | bytes 13824 | tf_op jit(solution)/shard_map/all_gather | solution.py:39
  293.1 0.5 divide_subtract_fusion
  293.6 8.8 %fusion.6 = f32[128,19008]{0,1:T(8,128)} fusion(pred[128,19008]{0,1:T(8,128)(4,1)S(1)} %get-tuple-element.22, f32[4,128,4752]{1,2,0:T(8,128)} %copy-done, f32[128]{0:T(128)S(1)} %get-tuple-element.19), kind=kLoop, calls=%fused_computation.13 | loop fusion | flops 4866048 | bytes 21897728 | tf_op jit(solution)/shard_map/jit(_where)/select_n | solution.py:32
  (9 shorter events, 0.1 us)
Async XLA Ops:
  7.2 33.1 %all-gather.5.cloned.1.call-start = ((), (), s32[]{:S(2)}) async-start(), calls=%async_computation.2 | async-start | bytes 1310720 | tf_op jit(solution)/shard_map/all_gather | solution.py:72
  7.9 88.0 %all-gather.7.cloned.1.call-start = ((), (), s32[]{:S(2)}) async-start(), calls=%async_computation.3 | async-start | bytes 9437184 | tf_op jit(solution)/shard_map/all_gather | solution.py:74
  145.9 11.8 %all-to-all-start.1 = ((f32[4,128,2]{1,2,0:T(2,128)}), f32[4,128,2]{1,2,0:T(2,128)S(1)}, u32[]{:S(2)}, u32[]{:S(2)}) async-start(f32[4,128,2]{1,2,0:T(2,128)} %pad_maximum_fusion), calls=%async_computation.1 | async-start | bytes 8192 | tf_op jit(solution)/shard_map/all_to_all | solution.py:66
  150.5 12.6 %copy-start.1 = (s32[2048,8]{0,1:T(8,128)S(1)}, s32[2048,8]{0,1:T(8,128)}, u32[]{:S(2)}) copy-start(s32[2048,8]{0,1:T(8,128)} %param.9) | copy-start | bytes 196612
  157.7 113.2 %all-to-all-start = ((s16[4,128,4752]{1,2,0:T(8,128)(2,1)}), s16[4,128,4752]{1,2,0:T(8,128)(2,1)}, u32[]{:S(2)}, u32[]{:S(2)}) async-start(s16[4,128,4752]{1,2,0:T(8,128)(2,1)} %copy_bitcast_fusion), calls=%async_computation | async-start | bytes 9732096 | tf_op jit(solution)/shard_map/all_to_all | solution.py:65
  162.9 112.3 %copy-start.2 = (s32[19008]{0:T(1024)S(1)}, s32[19008]{0:T(1024)}, u32[]{:S(2)}) copy-start(s32[19008]{0:T(1024)} %param.8) | copy-start | bytes 228100
  275.2 6.1 %copy-start = (f32[4,128,4752]{1,2,0:T(8,128)}, f32[4,128,4752]{1,2,0:T(8,128)S(1)}, u32[]{:S(2)}) copy-start(f32[4,128,4752]{1,2,0:T(8,128)S(1)} %multiply_add_fusion) | copy-start | bytes 29196292
Sparse Core Ops, SparseCore 0:
  9.5 30.6 all-gather.4
  42.2 53.6 all-gather.6
where the time goes:
time: 310 us; the launch traced here: 309 us
  waiting for transfers between devices  194 us (63%)
  matrix products  55.4 us (18%)
  other arithmetic  25.4 us (8%)
  between operations  14.2 us (5%)
  starting transfers between devices  9.88 us (3%)
  blocking collectives  8.87 us (3%)
    all_to_all x1, waiting for transfers between devices, to_row_groups(): codes = lax.all_to_all(codes.reshape(groups, own, columns), 'rows', 0, 0)  106 us
    all_gather x1, waiting for transfers between devices, on_device(): lax.all_gather(all_rows, 'vocab', axis=1, tiled=True)  55.5 us
    dot_general x1, matrix products, on_device(): jnp.dot(lax.all_gather(all_rows, 'vocab', axis=1, tiled=True), head, pref...  49.4 us
    all_gather x1, waiting for transfers between devices, on_device(): all_rows = lax.all_gather(hidden, 'rows', axis=0, tiled=True)  32.3 us
    all_gather x1, blocking collectives, vocab_stats(): lax.all_gather(jnp.stack([own_peak, own_total, own_weighted]), 'vocab', a...  8.87 us
    select_n x1, other arithmetic, finish(): log_probs = jnp.where(allowed, logits - norm_log[:, None], 0.0)  8.82 us
    reshape x1, other arithmetic, to_row_groups(): codes = lax.all_to_all(codes.reshape(groups, own, columns), 'rows', 0, 0)  7.23 us
  transfers between devices with their start and end apart: 4, of which 3 were waited for; matrix products, arithmetic and copies ran while one was open for 3% of the time, Pallas kernels for 0%

commit v1 on v0

--- a/solution.py
+++ b/solution.py
@@ -71,7 +71,7 @@
 def on_device(hidden, head, states, class_of, table):
     all_rows = lax.all_gather(hidden, "rows", axis=0, tiled=True)
     logits = jnp.dot(
-        lax.all_gather(all_rows, "vocab", axis=1, tiled=True),
+        jnp.concatenate(lax.all_gather(all_rows, "vocab"), axis=1),
         head,
         preferred_element_type=jnp.float32,
     )

time: 310 us -> 322 us (1.039)
  local copies, waits for them, and re-layouts: 1.13 us -> 12.5 us
    reshape x0 -> x1, local copies, waits for them, and re-layouts: none -> 11.4 us  [on_device(): jnp.concatenate(lax.all_gather(all_rows, 'vocab'), axis=1)]
where the time goes in v1:
time: 322 us; the launch traced here: 321 us
  waiting for transfers between devices  194 us (60%)
  matrix products  55.6 us (17%)
  other arithmetic  25.4 us (8%)
  between operations  14.2 us (4%)
  local copies, waits for them, and re-layouts  12.5 us (4%)
  starting transfers between devices  9.87 us (3%)
  blocking collectives  8.87 us (3%)
    all_to_all x1, waiting for transfers between devices, to_row_groups(): codes = lax.all_to_all(codes.reshape(groups, own, columns), 'rows', 0, 0)  106 us
    all_gather x1, waiting for transfers between devices, on_device(): lax.all_gather(all_rows, 'vocab')  55.5 us
    dot_general x1, matrix products, on_device(): jnp.dot(jnp.concatenate(lax.all_gather(all_rows, 'vocab'), axis=1), head,...  49.5 us
    all_gather x1, waiting for transfers between devices, on_device(): all_rows = lax.all_gather(hidden, 'rows', axis=0, tiled=True)  32.3 us
    reshape x1, local copies, waits for them, and re-layouts, on_device(): jnp.concatenate(lax.all_gather(all_rows, 'vocab'), axis=1)  11.4 us
    all_gather x1, blocking collectives, vocab_stats(): lax.all_gather(jnp.stack([own_peak, own_total, own_weighted]), 'vocab', a...  8.87 us
    select_n x1, other arithmetic, finish(): log_probs = jnp.where(allowed, logits - norm_log[:, None], 0.0)  8.82 us
    reshape x1, other arithmetic, to_row_groups(): codes = lax.all_to_all(codes.reshape(groups, own, columns), 'rows', 0, 0)  7.23 us
  transfers between devices with their start and end apart: 4, of which 3 were waited for; matrix products, arithmetic and copies ran while one was open for 3% of the time, Pallas kernels for 0%

profile of v1, /device:TPU:0, one launch (start us, length us, event | category | flops | bytes accessed | tf_op | source)
XLA Modules:
  0.0 320.9 jit_solution(5755598101429050182)
XLA Ops:
  7.2 0.0 all-gather.6.cloned.1.call-start
  7.2 0.7 all-gather.6.cloned.1.call-update
  7.9 0.0 all-gather.8.cloned.1.call-start
  7.9 32.3 %all-gather.6.cloned.1.call-done = bf16[512,1024]{1,0:T(8,128)(2,1)} async-done(((bf16[128,1024]{1,0:T(8,128)(2,1)}), bf16[512,1024]{1,0:T(8,128)(2,1)}) %all-gather.6.cloned.1.call-update) | async-done | bytes 1048592 | tf_op jit(solution)/shard_map/all_gather | solution.py:72
  40.3 0.0 all-gather.8.cloned.1.call-update
  40.3 55.5 %all-gather.8.cloned.1.call-done = bf16[4096,1024]{1,0:T(8,128)(2,1)} async-done(((bf16[512,1024]{1,0:T(8,128)(2,1)}), bf16[4096,1024]{1,0:T(8,128)(2,1)}) %all-gather.8.cloned.1.call-update) | async-done | bytes 8388624 | tf_op jit(solution)/shard_map/all_gather | solution.py:74
  95.8 11.4 %copy.24 = bf16[512,8,1024]{0,2,1:T(8,128)(2,1)} copy(bf16[512,8,1024]{2,0,1:T(8,128)(2,1)} %bitcast.55) | data formatting | bytes 16777216 | tf_op jit(solution)/shard_map/reshape | solution.py:74
  107.3 49.5 %fusion.10 = (f32[512]{0:T(512)S(1)}, f32[512]{0:T(512)S(1)}, f32[512,4752]{0,1:T(8,128)}) fusion(bf16[8192,4752]{0,1:T(8,128)(2,1)} %param.6, bf16[512,8192]{0,1:T(8,128)(2,1)} %bitcast.56), kind=kOutput, calls=%fused_computation.36 | convolution fusion | flops 39867531264 | bytes 95981568 | tf_op jit(solution)/shard_map/dot_general | solution.py:73
  156.8 0.6 pad_maximum_fusion
  157.4 4.6 %all-to-all-start.1 = ((f32[4,128,2]{1,2,0:T(2,128)}), f32[4,128,2]{1,2,0:T(2,128)S(1)}, u32[]{:S(2)}, u32[]{:S(2)}) async-start(f32[4,128,2]{1,2,0:T(2,128)} %pad_maximum_fusion), calls=%async_computation.1 | async-start | bytes 8192 | tf_op jit(solution)/shard_map/all_to_all | solution.py:66
  162.0 0.0 copy-start.1
  162.0 7.2 %copy_bitcast_fusion = s16[4,128,4752]{1,2,0:T(8,128)(2,1)} fusion(f32[512,4752]{0,1:T(8,128)} %get-tuple-element.20, f32[512]{0:T(512)S(1)} %get-tuple-element.16, f32[512]{0:T(512)S(1)} %get-tuple-element.17), kind=kLoop, calls=%fused_computation.17 | loop fusion | flops 12165120 | bytes 14602240 | tf_op jit(solution)/shard_map/reshape | solution.py:65
  169.2 0.0 all-to-all-done.1
  169.2 5.2 %all-to-all-start = ((s16[4,128,4752]{1,2,0:T(8,128)(2,1)}), s16[4,128,4752]{1,2,0:T(8,128)(2,1)}, u32[]{:S(2)}, u32[]{:S(2)}) async-start(s16[4,128,4752]{1,2,0:T(8,128)(2,1)} %copy_bitcast_fusion), calls=%async_computation | async-start | bytes 9732096 | tf_op jit(solution)/shard_map/all_to_all | solution.py:65
  174.5 0.0 copy-start.2
  174.5 0.1 shift_right_arithmetic.23
  174.6 0.0 copy-done.1
  174.6 0.3 copy.22
  174.9 0.8 compare_and_fusion
  175.7 0.6 gather_fusion
  176.3 0.1 broadcast_select_fusion
  176.5 0.1 fusion.9
  176.6 105.9 %all-to-all-done = s16[4,128,4752]{1,2,0:T(8,128)(2,1)} async-done(((s16[4,128,4752]{1,2,0:T(8,128)(2,1)}), s16[4,128,4752]{1,2,0:T(8,128)(2,1)}, u32[]{:S(2)}, u32[]{:S(2)}) %all-to-all-start) | async-done | bytes 4866080 | tf_op jit(solution)/shard_map/all_to_all | solution.py:65
  282.5 4.3 %multiply_add_fusion = f32[4,128,4752]{1,2,0:T(8,128)S(1)} fusion(s16[4,128,4752]{1,2,0:T(8,128)(2,1)} %all-to-all-done, f32[4,128]{1,0:T(4,128)S(1)} %bitcast.63, f32[4,128]{1,0:T(4,128)S(1)} %bitcast.62), kind=kLoop, calls=%fused_computation.14 | loop fusion | flops 7299072 | bytes 14602240 | tf_op jit(solution)/shard_map/add | solution.py:67
  286.7 0.0 copy-done.2
  286.7 0.0 copy-start
  286.8 6.1 %fusion.1 = (f32[128]{0:T(128)S(1)}, pred[128,19008]{0,1:T(8,128)(4,1)S(1)}) fusion(f32[4,128,4752]{1,2,0:T(8,128)S(1)} %multiply_add_fusion, bf16[128,256]{0,1:T(8,128)(2,1)S(1)} %fusion.9, s32[19008]{0:T(1024)S(1)} %copy-done.2), kind=kOutput, calls=%fused_computation.8 | convolution fusion | flops 1257873280 | bytes 12307200 | tf_op jit(solution)/shard_map/dot_general | solution.py:18
  292.8 0.0 copy-done
  292.8 2.9 fusion.4
  295.8 8.9 %all-gather.2 = f32[8,3,128]{2,1,0:T(4,128)S(1)} all-gather(f32[1,3,128]{2,1,0:T(4,128)S(1)} %maximum_bitcast_fusion), channel_id=3, replica_groups=mesh['rows'=4,'vocab'=8] {'vocab'}, dimensions={0}, use_global_device_ids=true | all-gather | bytes 13824 | tf_op jit(solution)/shard_map/all_gather | solution.py:39
  304.7 0.5 divide_subtract_fusion
  305.2 8.8 %fusion.6 = f32[128,19008]{0,1:T(8,128)} fusion(pred[128,19008]{0,1:T(8,128)(4,1)S(1)} %get-tuple-element.22, f32[4,128,4752]{1,2,0:T(8,128)} %copy-done, f32[128]{0:T(128)S(1)} %get-tuple-element.19), kind=kLoop, calls=%fused_computation.13 | loop fusion | flops 4866048 | bytes 21897728 | tf_op jit(solution)/shard_map/jit(_where)/select_n | solution.py:32
  (9 shorter events, 0.1 us)
Async XLA Ops:
  7.2 33.1 %all-gather.6.cloned.1.call-start = ((), (), s32[]{:S(2)}) async-start(), calls=%async_computation.2 | async-start | bytes 1310720 | tf_op jit(solution)/shard_map/all_gather | solution.py:72
  7.9 87.9 %all-gather.8.cloned.1.call-start = ((), (), s32[]{:S(2)}) async-start(), calls=%async_computation.3 | async-start | bytes 9437184 | tf_op jit(solution)/shard_map/all_gather | solution.py:74
  157.4 11.8 %all-to-all-start.1 = ((f32[4,128,2]{1,2,0:T(2,128)}), f32[4,128,2]{1,2,0:T(2,128)S(1)}, u32[]{:S(2)}, u32[]{:S(2)}) async-start(f32[4,128,2]{1,2,0:T(2,128)} %pad_maximum_fusion), calls=%async_computation.1 | async-start | bytes 8192 | tf_op jit(solution)/shard_map/all_to_all | solution.py:66
  162.0 12.6 %copy-start.1 = (s32[2048,8]{0,1:T(8,128)S(1)}, s32[2048,8]{0,1:T(8,128)}, u32[]{:S(2)}) copy-start(s32[2048,8]{0,1:T(8,128)} %param.9) | copy-start | bytes 196612
  169.2 113.2 %all-to-all-start = ((s16[4,128,4752]{1,2,0:T(8,128)(2,1)}), s16[4,128,4752]{1,2,0:T(8,128)(2,1)}, u32[]{:S(2)}, u32[]{:S(2)}) async-start(s16[4,128,4752]{1,2,0:T(8,128)(2,1)} %copy_bitcast_fusion), calls=%async_computation | async-start | bytes 9732096 | tf_op jit(solution)/shard_map/all_to_all | solution.py:65
  174.5 112.3 %copy-start.2 = (s32[19008]{0:T(1024)S(1)}, s32[19008]{0:T(1024)}, u32[]{:S(2)}) copy-start(s32[19008]{0:T(1024)} %param.8) | copy-start | bytes 228100
  286.7 6.1 %copy-start = (f32[4,128,4752]{1,2,0:T(8,128)}, f32[4,128,4752]{1,2,0:T(8,128)S(1)}, u32[]{:S(2)}) copy-start(f32[4,128,4752]{1,2,0:T(8,128)S(1)} %multiply_add_fusion) | copy-start | bytes 29196292
Sparse Core Ops, SparseCore 0:
  9.5 30.6 all-gather.5
  42.2 53.6 all-gather.7
